TPU v7x, 32 devices: a whole 2x2x4 slice. The times are simulated.
32 devices in a mesh: freq: 8 (over y, x, core), gz: 4 (over z).
Axes of the slice: x: 2, y: 2, z: 4, core: 2. Of those that a mesh axis runs over, the one named last changes fastest.
Arguments:
- displacement: float32 [8, 2, 3, 16, 64, 128], P('freq', None, None, 'gz'), may hold values from -6 to 6
- freq_index: int32 [8], P('freq'), may hold values from 0 to 7
- tissue: int32 [16, 64, 128], P('gz'), may hold values from 0 to 1, as said below
Outputs:
- modulus: float32 [2, 16, 64, 128], P(None, 'gz')
- residual: float32 [2, 16, 64, 128], P(None, 'gz')
Inputs may be any that keep to these rules, and one draw needn't show every extreme that they name: 0 outside tissue, 1 inside; the share of tissue rises along z from about 0.15 to about 0.95.
All inputs are finite; a program needn't handle non-finite values.
Results may differ from a plain program's by a relative error of at most 0.0003.
Values sent between devices are 32-bit elements; how exact they have to be, the bound alone decides.
A program may use at most 64 MiB of HBM per device.

v0:
```python
import jax
import jax.numpy as jnp
from jax import lax
from jax.sharding import PartitionSpec as P

ITERS = 2


DAMPING = 0.05


def passed_along(array, axis, by):
    peers = lax.axis_size(axis)
    pairs = [(i, i + by) for i in range(peers) if 0 <= i + by < peers]
    return lax.ppermute(array, axis, pairs)


def zero_plane(field, spatial):
    return jnp.zeros_like(lax.slice_in_dim(field, 0, 1, axis=spatial))


def ahead(field, spatial, tail):
    moved = lax.slice_in_dim(field, 1, field.shape[spatial], axis=spatial)
    return jnp.concatenate([moved, tail], axis=spatial)


def behind(field, spatial, head):
    moved = lax.slice_in_dim(field, 0, field.shape[spatial] - 1, axis=spatial)
    return jnp.concatenate([head, moved], axis=spatial)


def gradients(field):
    above = passed_along(field[:, :, :1], "gz", -1)
    grads = [ahead(field, 2, above) - field]
    for spatial in (3, 4):
        grads.append(ahead(field, spatial, zero_plane(field, spatial)) - field)
    return grads


def forward(modulus, grads):
    total = None
    for spatial, grad in zip((2, 3, 4), grads):
        real = modulus[0] * grad[0] - modulus[1] * grad[1]
        imag = modulus[0] * grad[1] + modulus[1] * grad[0]
        flux = jnp.stack([real, imag])
        if spatial == 2:
            head = passed_along(flux[:, :, -1:], "gz", 1)
        else:
            head = zero_plane(flux, spatial)
        term = flux - behind(flux, spatial, head)
        total = term if total is None else total + term
    return total


def adjoint(values, grads):
    real = None
    imag = None
    for spatial, grad in zip((2, 3, 4), grads):
        if spatial == 2:
            tail = passed_along(values[:, :, :1], "gz", -1)
        else:
            tail = zero_plane(values, spatial)
        diff = values - ahead(values, spatial, tail)
        part_real = jnp.sum(grad[0] * diff[0] + grad[1] * diff[1], axis=0)
        part_imag = jnp.sum(grad[0] * diff[1] - grad[1] * diff[0], axis=0)
        real = part_real if real is None else real + part_real
        imag = part_imag if imag is None else imag + part_imag
    return jnp.stack([real, imag])


def body(displacement, freq_index, tissue):
    field = displacement[0]
    weight = tissue.astype(jnp.float32)
    kappa = 0.2 * (freq_index[0] + 1).astype(jnp.float32)
    grads = gradients(field)
    right_local = adjoint(weight * (-kappa * field), grads)

    def summed_all(local):
        return lax.psum(local, "freq")

    def inner(first, second):
        return lax.psum(jnp.sum(first * second), "gz")

    residual = summed_all(right_local)
    modulus = jnp.zeros_like(residual)
    direction = residual
    norm_now = inner(residual, residual)
    for iteration in range(ITERS):
        image = summed_all(adjoint(weight * forward(direction, grads), grads)) + DAMPING * direction
        step_size = norm_now / inner(direction, image)
        modulus = modulus + step_size * direction
        residual = residual - step_size * image
        norm_next = inner(residual, residual)
        direction = residual + norm_next / norm_now * direction
        norm_now = norm_next
    return (modulus, residual)


def solution(mesh):
    placed = (P("freq", None, None, "gz", None, None), P("freq"), P("gz", None, None))
    return jax.shard_map(
        body,
        mesh=mesh,
        in_specs=placed,
        out_specs=(P(None, "gz", None, None), P(None, "gz", None, None)),
        check_vma=False,
    )
```

profile of v0, /device:TPU:0, one launch (start us, length us, event | category | flops | bytes accessed | tf_op | source)
XLA Modules:
  0.0 272.9 jit_solution(10253733803819380597)
XLA Ops:
  7.2 1.0 slice.301
  8.2 1.3 collective-permute-start
  9.5 1.1 slice.300
  11.9 6.2 %collective-permute-done = f32[2,3,1,64,128]{4,3,2,1,0:T(8,128)S(1)} collective-permute-done((f32[2,3,1,64,128]{4,3,2,1,0:T(8,128)S(1)}, f32[2,3,1,64,128]{4,3,2,1,0:T(8,128)S(1)}, u32[]{:S(2)}, u32[]{:S(2)}) %collective-permute-start) | collective-permute-done | bytes 196640 | tf_op jit(solution)/shard_map/ppermute | solution.py:15
  18.5 1.3 collective-permute-start.1
  20.3 6.2 %collective-permute-done.1 = f32[2,3,1,64,128]{4,3,2,1,0:T(8,128)S(1)} collective-permute-done((f32[2,3,1,64,128]{4,3,2,1,0:T(8,128)S(1)}, f32[2,3,1,64,128]{4,3,2,1,0:T(8,128)S(1)}, u32[]{:S(2)}, u32[]{:S(2)}) %collective-permute-start.1) | collective-permute-done | bytes 196640 | tf_op jit(solution)/shard_map/ppermute | solution.py:15
  28.4 54.1 %all-reduce.17.cloned.1.call-done = f32[2,4,64,128]{3,2,1,0:T(8,128)} async-done(((f32[2,4,64,128]{3,2,1,0:T(8,128)}), f32[2,4,64,128]{3,2,1,0:T(8,128)}) %all-reduce.17.cloned.1.call-update) | async-done | bytes 262160 | tf_op jit(solution)/shard_map/psum | solution.py:79
  82.4 1.0 slice_bitcast_fusion.3
  83.8 3.4 %collective-permute-start.2 = (f32[2,3,1,64,128]{4,3,2,1,0:T(8,128)S(1)}, f32[2,3,1,64,128]{4,3,2,1,0:T(8,128)S(1)}, u32[]{:S(2)}, u32[]{:S(2)}) collective-permute-start(f32[2,3,1,64,128]{4,3,2,1,0:T(8,128)S(1)} %fusion.19), channel_id=1, source_target_pairs={{0,1},{1,2},{2,3},{4,5},{5,6},{6,7},{8,9},{9,10},{10,11},{12,13},{... | collective-permute-start | bytes 589832 | tf_op jit(solution)/shard_map/ppermute | solution.py:15
  87.4 3.1 %collective-permute-done.2 = f32[2,3,1,64,128]{4,3,2,1,0:T(8,128)S(1)} collective-permute-done((f32[2,3,1,64,128]{4,3,2,1,0:T(8,128)S(1)}, f32[2,3,1,64,128]{4,3,2,1,0:T(8,128)S(1)}, u32[]{:S(2)}, u32[]{:S(2)}) %collective-permute-start.2) | collective-permute-done | bytes 196640 | tf_op jit(solution)/shard_map/ppermute | solution.py:15
  91.0 1.3 collective-permute-start.3
  92.7 6.3 %collective-permute-done.3 = f32[2,3,1,64,128]{4,3,2,1,0:T(8,128)S(1)} collective-permute-done((f32[2,3,1,64,128]{4,3,2,1,0:T(8,128)S(1)}, f32[2,3,1,64,128]{4,3,2,1,0:T(8,128)S(1)}, u32[]{:S(2)}, u32[]{:S(2)}) %collective-permute-start.3) | collective-permute-done | bytes 196640 | tf_op jit(solution)/shard_map/ppermute | solution.py:15
  100.8 53.0 %all-reduce.19.cloned.1.call-done = f32[2,4,64,128]{3,2,1,0:T(8,128)} async-done(((f32[2,4,64,128]{3,2,1,0:T(8,128)}), f32[2,4,64,128]{3,2,1,0:T(8,128)}) %all-reduce.19.cloned.1.call-update) | async-done | bytes 262160 | tf_op jit(solution)/shard_map/psum | solution.py:79
  153.8 1.7 multiply_reduce_fusion.2
  155.5 12.3 %all-reduce.12 = (f32[]{:T(128)}, f32[]{:T(128)}) all-reduce(f32[]{:T(128)} %get-tuple-element.21, f32[]{:T(128)} %get-tuple-element.20), channel_id=1, replica_groups=mesh['freq'=8,'gz'=4] {'gz'}, use_global_device_ids=true, to_apply=%region_8.0 | all-reduce | flops 2 | bytes 16 | tf_op jit(solution)/shard_map/psum | solution.py:82
  169.8 9.0 %psum.53 = f32[]{:T(128)} all-reduce(f32[]{:T(128)} %multiply_reduce_fusion.1), channel_id=1, replica_groups=mesh['freq'=8,'gz'=4] {'gz'}, use_global_device_ids=true, to_apply=%region_19.0 | all-reduce | flops 1 | bytes 8 | tf_op jit(solution)/shard_map/psum | solution.py:82
  180.6 3.9 %collective-permute-start.4 = (f32[2,3,1,64,128]{4,3,2,1,0:T(8,128)S(1)}, f32[2,3,1,64,128]{4,3,2,1,0:T(8,128)S(1)}, u32[]{:S(2)}, u32[]{:S(2)}) collective-permute-start(f32[2,3,1,64,128]{4,3,2,1,0:T(8,128)S(1)} %fusion.18), channel_id=1, source_target_pairs={{0,1},{1,2},{2,3},{4,5},{5,6},{6,7},{8,9},{9,10},{10,11},{12,13},{... | collective-permute-start | bytes 589832 | tf_op jit(solution)/shard_map/ppermute | solution.py:15
  184.7 2.9 %collective-permute-done.4 = f32[2,3,1,64,128]{4,3,2,1,0:T(8,128)S(1)} collective-permute-done((f32[2,3,1,64,128]{4,3,2,1,0:T(8,128)S(1)}, f32[2,3,1,64,128]{4,3,2,1,0:T(8,128)S(1)}, u32[]{:S(2)}, u32[]{:S(2)}) %collective-permute-start.4) | collective-permute-done | bytes 196640 | tf_op jit(solution)/shard_map/ppermute | solution.py:15
  188.2 1.3 collective-permute-start.5
  189.9 6.3 %collective-permute-done.5 = f32[2,3,1,64,128]{4,3,2,1,0:T(8,128)S(1)} collective-permute-done((f32[2,3,1,64,128]{4,3,2,1,0:T(8,128)S(1)}, f32[2,3,1,64,128]{4,3,2,1,0:T(8,128)S(1)}, u32[]{:S(2)}, u32[]{:S(2)}) %collective-permute-start.5) | collective-permute-done | bytes 196640 | tf_op jit(solution)/shard_map/ppermute | solution.py:15
  198.0 52.2 %all-reduce.21.cloned.1.call-done = f32[2,4,64,128]{3,2,1,0:T(8,128)} async-done(((f32[2,4,64,128]{3,2,1,0:T(8,128)}), f32[2,4,64,128]{3,2,1,0:T(8,128)}) %all-reduce.21.cloned.1.call-update) | async-done | bytes 262160 | tf_op jit(solution)/shard_map/psum | solution.py:79
  250.2 1.7 multiply_reduce_fusion
  251.9 12.3 %psum.55 = f32[]{:T(128)} all-reduce(f32[]{:T(128)} %multiply_reduce_fusion), channel_id=1, replica_groups=mesh['freq'=8,'gz'=4] {'gz'}, use_global_device_ids=true, to_apply=%region_28.0 | all-reduce | flops 1 | bytes 8 | tf_op jit(solution)/shard_map/psum | solution.py:82
  265.5 0.9 multiply_subtract_fusion.6
  (67 shorter events, 10.3 us)
Async XLA Ops:
  7.2 75.3 %all-reduce.17.cloned.1.call-start = ((), (), s32[]{:S(2)}) async-start(), calls=%async_computation | async-start | bytes 524288 | tf_op jit(solution)/shard_map/psum | solution.py:79
  7.2 3.4 %copy-start = (f32[1,2,3,4,64,128]{5,4,3,2,1,0:T(8,128)S(1)}, f32[1,2,3,4,64,128]{5,4,3,2,1,0:T(8,128)}, u32[]{:S(2)}) copy-start(f32[1,2,3,4,64,128]{5,4,3,2,1,0:T(8,128)} %param.3) | copy-start | bytes 2359300
  8.2 9.9 %collective-permute-start = (f32[2,3,1,64,128]{4,3,2,1,0:T(8,128)S(1)}, f32[2,3,1,64,128]{4,3,2,1,0:T(8,128)S(1)}, u32[]{:S(2)}, u32[]{:S(2)}) collective-permute-start(f32[2,3,1,64,128]{4,3,2,1,0:T(8,128)S(1)} %slice.301), channel_id=1, source_target_pairs={{1,0},{2,1},{3,2},{5,4},{6,5},{7,6},{9,8},{10,9},{11,10},{13,12},{... | collective-permute-start | bytes 589832 | tf_op jit(solution)/shard_map/ppermute | solution.py:15
  10.9 0.9 copy-start.4
  18.5 8.0 %collective-permute-start.1 = (f32[2,3,1,64,128]{4,3,2,1,0:T(8,128)S(1)}, f32[2,3,1,64,128]{4,3,2,1,0:T(8,128)S(1)}, u32[]{:S(2)}, u32[]{:S(2)}) collective-permute-start(f32[2,3,1,64,128]{4,3,2,1,0:T(8,128)S(1)} %slice.304), channel_id=1, source_target_pairs={{1,0},{2,1},{3,2},{5,4},{6,5},{7,6},{9,8},{10,9},{11,10},{13,12},{... | collective-permute-start | bytes 589832 | tf_op jit(solution)/shard_map/ppermute | solution.py:15
  28.3 125.5 %all-reduce.19.cloned.1.call-start = ((), (), s32[]{:S(2)}) async-start(), calls=%async_computation.1 | async-start | bytes 524288 | tf_op jit(solution)/shard_map/psum | solution.py:79
  83.8 6.7 %collective-permute-start.2 = (f32[2,3,1,64,128]{4,3,2,1,0:T(8,128)S(1)}, f32[2,3,1,64,128]{4,3,2,1,0:T(8,128)S(1)}, u32[]{:S(2)}, u32[]{:S(2)}) collective-permute-start(f32[2,3,1,64,128]{4,3,2,1,0:T(8,128)S(1)} %fusion.19), channel_id=1, source_target_pairs={{0,1},{1,2},{2,3},{4,5},{5,6},{6,7},{8,9},{9,10},{10,11},{12,13},{... | collective-permute-start | bytes 589832 | tf_op jit(solution)/shard_map/ppermute | solution.py:15
  91.0 8.0 %collective-permute-start.3 = (f32[2,3,1,64,128]{4,3,2,1,0:T(8,128)S(1)}, f32[2,3,1,64,128]{4,3,2,1,0:T(8,128)S(1)}, u32[]{:S(2)}, u32[]{:S(2)}) collective-permute-start(f32[2,3,1,64,128]{4,3,2,1,0:T(8,128)S(1)} %slice.331), channel_id=1, source_target_pairs={{1,0},{2,1},{3,2},{5,4},{6,5},{7,6},{9,8},{10,9},{11,10},{13,12},{... | collective-permute-start | bytes 589832 | tf_op jit(solution)/shard_map/ppermute | solution.py:15
  100.8 53.0 %copy-start.1 = (f32[2,4,64,128]{3,2,1,0:T(8,128)S(1)}, f32[2,4,64,128]{3,2,1,0:T(8,128)}, u32[]{:S(2)}) copy-start(f32[2,4,64,128]{3,2,1,0:T(8,128)} %all-reduce.17.cloned.1.call-done) | copy-start | bytes 786436
  100.8 149.4 %all-reduce.21.cloned.1.call-start = ((), (), s32[]{:S(2)}) async-start(), calls=%async_computation.2 | async-start | bytes 524288 | tf_op jit(solution)/shard_map/psum | solution.py:79
  153.8 15.3 %copy-start.2 = (f32[2,4,64,128]{3,2,1,0:T(8,128)S(1)}, f32[2,4,64,128]{3,2,1,0:T(8,128)}, u32[]{:S(2)}) copy-start(f32[2,4,64,128]{3,2,1,0:T(8,128)} %all-reduce.19.cloned.1.call-done) | copy-start | bytes 786436
  180.6 7.1 %collective-permute-start.4 = (f32[2,3,1,64,128]{4,3,2,1,0:T(8,128)S(1)}, f32[2,3,1,64,128]{4,3,2,1,0:T(8,128)S(1)}, u32[]{:S(2)}, u32[]{:S(2)}) collective-permute-start(f32[2,3,1,64,128]{4,3,2,1,0:T(8,128)S(1)} %fusion.18), channel_id=1, source_target_pairs={{0,1},{1,2},{2,3},{4,5},{5,6},{6,7},{8,9},{9,10},{10,11},{12,13},{... | collective-permute-start | bytes 589832 | tf_op jit(solution)/shard_map/ppermute | solution.py:15
  188.2 8.0 %collective-permute-start.5 = (f32[2,3,1,64,128]{4,3,2,1,0:T(8,128)S(1)}, f32[2,3,1,64,128]{4,3,2,1,0:T(8,128)S(1)}, u32[]{:S(2)}, u32[]{:S(2)}) collective-permute-start(f32[2,3,1,64,128]{4,3,2,1,0:T(8,128)S(1)} %slice.351), channel_id=1, source_target_pairs={{1,0},{2,1},{3,2},{5,4},{6,5},{7,6},{9,8},{10,9},{11,10},{13,12},{... | collective-permute-start | bytes 589832 | tf_op jit(solution)/shard_map/ppermute | solution.py:15
  250.2 15.3 %copy-start.3 = (f32[2,4,64,128]{3,2,1,0:T(8,128)S(1)}, f32[2,4,64,128]{3,2,1,0:T(8,128)}, u32[]{:S(2)}) copy-start(f32[2,4,64,128]{3,2,1,0:T(8,128)} %all-reduce.21.cloned.1.call-done) | copy-start | bytes 786436
Sparse Core Ops, SparseCore 0:
  28.4 53.9 all-reduce.16
  100.9 52.8 all-reduce.18
  198.1 52.0 all-reduce.20
where the time goes:
time: 273 us
  waiting for transfers between devices  190 us (70%)
  blocking collectives  33.6 us (12%)
  between operations  18.7 us (7%)
  starting transfers between devices  12.6 us (5%)
  other arithmetic  12.6 us (5%)
  local copies, waits for them, and re-layouts  4.88 us (2%)
    psum x3, waiting for transfers between devices, summed_all(): return lax.psum(local, 'freq')  159 us
    psum x3, blocking collectives, inner(): return lax.psum(jnp.sum(first * second), 'gz')  33.6 us
    ppermute x6, waiting for transfers between devices, passed_along(): return lax.ppermute(array, axis, pairs)  31.2 us
    ppermute x6, starting transfers between devices, passed_along(): return lax.ppermute(array, axis, pairs)  12.5 us
  transfers between devices with their start and end apart: 9, of which 9 were waited for; matrix products, arithmetic and copies ran while one was open for 1% of the time, Pallas kernels for 0%

commit v1 on v0

v1 whole, which is shorter than its diff:
```python
import functools

import jax
import jax.numpy as jnp
from jax import lax
from jax.experimental import pallas as pl
from jax.experimental.pallas import tpu as pltpu
from jax.sharding import PartitionSpec as P

MESH = pl.DeviceIdType.MESH
DAMPING = 0.05
ZZ, Z0, ZY, ZX = 0, 1, 3, 5
YY, Y0, YX = 7, 8, 10
CC, C0X, XX = 12, 13, 15
FIELDS = 16


def shifted_up(array, tail):
    rows = array.shape[0]
    if rows % 8 == 0:
        last = lax.broadcasted_iota(jnp.int32, array.shape, 0) == rows - 1
        return jnp.where(last, jnp.broadcast_to(tail, array.shape), pltpu.roll(array, rows - 1, 0))
    return jnp.concatenate([array[1:], tail], axis=0)


def shifted_down(array, head):
    rows = array.shape[0]
    if rows % 8 == 0:
        first = lax.broadcasted_iota(jnp.int32, array.shape, 0) == 0
        return jnp.where(first, jnp.broadcast_to(head, array.shape), pltpu.roll(array, 1, 0))
    return jnp.concatenate([head, array[:-1]], axis=0)


def lane_next(array):
    return pltpu.roll(array, array.shape[1] - 1, 1)


def lane_prev(array):
    return pltpu.roll(array, 1, 1)


def mul(a, b):
    return a[0] * b[0] - a[1] * b[1], a[0] * b[1] + a[1] * b[0]


def cmul(a, b):
    return a[0] * b[0] + a[1] * b[1], a[0] * b[1] - a[1] * b[0]


def add(*terms):
    return sum(t[0] for t in terms[1:]) + terms[0][0], sum(t[1] for t in terms[1:]) + terms[0][1]


def scale(r, a):
    return r * a[0], r * a[1]


def kernel(nf, nz, u, tis, fi, mod_out, res_out,
           ubuf, hsrc, hbuf, zlo, zhi, wsrc, wz, macc, bacc, mz, ysrc, yp, gath, mlo, mloc, mhi, mhic,
           scs, scr, sgs, sgr,
           loc_s, main_s, main_r, halo_s, halo_r, flo_s, fhi_s, zlo_r, zhi_r, w_sem, mz_sem, yp_sem,
           ag_s, ag_r, pl_s, pl_r, sc_s, sc_r, sg_s, sg_r):
    f = lax.axis_index("freq")
    z = lax.axis_index("gz")
    _, comps, depth, _, rows, width = u.shape
    below, above = z > 0, z < nz - 1
    first, last = f > 0, f < nf - 1
    fnext, fprev = lax.rem(f + 1, nf), lax.rem(f + nf - 1, nf)
    zn, zp = z + 1, z - 1

    def remote(src, dst, ssem, rsem, df, dz):
        return pltpu.make_async_remote_copy(
            src_ref=src, dst_ref=dst, send_sem=ssem, recv_sem=rsem, device_id=(df, dz), device_id_type=MESH)

    barrier = pltpu.get_barrier_semaphore()

    def greet(df, dz):
        pl.semaphore_signal(barrier, inc=1, device_id=(df, dz), device_id_type=MESH)

    for k in range(1, nf):
        greet(lax.rem(f + k, nf), z)
    for k in range(1, nz):
        greet(f, lax.rem(z + k, nz))
    diag_up = jnp.logical_and(first, above)
    diag_down = jnp.logical_and(last, below)

    @pl.when(diag_up)
    def _():
        greet(f - 1, zn)

    @pl.when(diag_down)
    def _():
        greet(f + 1, zp)

    kappa = 0.2 * (fi[0] + 1).astype(jnp.float32)
    zero_row = jnp.zeros((1, width), jnp.float32)
    for d in range(nf):
        for p in range(2):
            for c in range(comps):
                for i in range(depth):
                    lo = u[p, c, i, d - 1, rows - 1:rows, :] if d > 0 else zero_row
                    hi = u[p, c, i, d + 1, 0:1, :] if d < nf - 1 else zero_row
                    hsrc[d, p * comps + c, i:i + 1, :] = lo
                    hsrc[d, p * comps + c, depth + i:depth + i + 1, :] = hi
        hsrc[d, 2 * comps] = jnp.full((2 * depth, width), kappa, jnp.float32)
    wsrc[...] = tis[0, f].astype(jnp.float32)

    @pl.when(jnp.logical_not(below))
    def _():
        zlo[...] = jnp.zeros_like(zlo)
        mlo[...] = jnp.zeros_like(mlo)

    @pl.when(jnp.logical_not(above))
    def _():
        zhi[...] = jnp.zeros_like(zhi)
        mhi[...] = jnp.zeros_like(mhi)
        wz[...] = jnp.zeros_like(wz)
        mz[...] = jnp.zeros_like(mz)

    @pl.when(jnp.logical_not(last))
    def _():
        yp[...] = jnp.zeros_like(yp)

    @pl.when(jnp.logical_not(diag_up))
    def _():
        mhic[...] = jnp.zeros_like(mhic)

    @pl.when(jnp.logical_not(diag_down))
    def _():
        mloc[...] = jnp.zeros_like(mloc)

    own_u = pltpu.make_async_copy(u.at[:, :, :, f], ubuf.at[f], loc_s.at[0])
    own_h = pltpu.make_async_copy(hsrc.at[f], hbuf.at[f], loc_s.at[1])
    own_u.start()
    own_h.start()
    macc[...] = jnp.zeros_like(macc)
    bacc[...] = jnp.zeros_like(bacc)

    pl.semaphore_wait(barrier, (nf - 1) + (nz - 1) + diag_up.astype(jnp.int32) + diag_down.astype(jnp.int32))

    def sends(d):
        return (remote(hsrc.at[d], hbuf.at[f], halo_s.at[d], halo_r.at[f], d, z),
                remote(u.at[:, :, :, d], ubuf.at[f], main_s.at[d], main_r.at[f], d, z))

    def arrivals(s):
        return (remote(hsrc.at[s], hbuf.at[s], halo_s.at[s], halo_r.at[s], s, z),
                remote(u.at[:, :, :, s], ubuf.at[s], main_s.at[s], main_r.at[s], s, z))

    for k in range(1, nf):
        for copy in sends(lax.rem(f + k, nf)):
            copy.start()

    w_copy = remote(wsrc, wz, w_sem.at[0], w_sem.at[1], f, zp)
    w_from = remote(wsrc, wz, w_sem.at[0], w_sem.at[1], f, zn)

    @pl.when(below)
    def _():
        w_copy.start()

    def forward_up(s):
        return remote(ubuf.at[s, :, :, depth - 1], zlo.at[s], flo_s.at[s], zlo_r.at[s], f, zn)

    def forward_down(s):
        return remote(ubuf.at[s, :, :, 0], zhi.at[s], fhi_s.at[s], zhi_r.at[s], f, zp)

    def from_below(s):
        return remote(ubuf.at[s, :, :, depth - 1], zlo.at[s], flo_s.at[s], zlo_r.at[s], f, zp)

    def from_above(s):
        return remote(ubuf.at[s, :, :, 0], zhi.at[s], fhi_s.at[s], zhi_r.at[s], f, zn)

    def forwards(s):
        @pl.when(above)
        def _():
            forward_up(s).start()

        @pl.when(below)
        def _():
            forward_down(s).start()

    own_u.wait()
    own_h.wait()
    forwards(f)

    @pl.when(above)
    def _():
        w_from.wait_recv()

    lane_last = lax.broadcasted_iota(jnp.int32, (rows, width), 1) == width - 1
    lane_first = lax.broadcasted_iota(jnp.int32, (rows, width), 1) == 0
    last_scale = jnp.where(last, 1.0, 0.0).astype(jnp.float32)

    def weight(i):
        return tis[i, f].astype(jnp.float32)

    def group(s):
        kap = hbuf[s, 2 * comps, 0:1, :]
        for i in range(depth):
            w = weight(i)
            w_z = weight(i + 1) if i + 1 < depth else wz[...]
            w_y = shifted_up(w, tis[i, fnext, 0:1, :].astype(jnp.float32) * last_scale)
            w_x = jnp.where(lane_last, 0.0, lane_next(w))
            tot = [None] * FIELDS
            right = None
            for c in range(comps):
                here, az, ay, ax, gz, gy, gx, uz, uy, ux = ([None, None] for _ in range(10))
                for p in range(2):
                    v = ubuf[s, p, c, i]
                    prev_z = ubuf[s, p, c, i - 1] if i > 0 else zlo[s, p, c]
                    next_z = ubuf[s, p, c, i + 1] if i + 1 < depth else zhi[s, p, c]
                    lo = hbuf[s, p * comps + c, i:i + 1, :]
                    hi = hbuf[s, p * comps + c, depth + i:depth + i + 1, :]
                    next_y = shifted_up(v, hi)
                    prev_y = shifted_down(v, lo)
                    next_x = jnp.where(lane_last, 0.0, lane_next(v))
                    prev_x = lane_prev(v)
                    here[p] = v
                    uz[p], uy[p], ux[p] = next_z, next_y, next_x
                    gz[p], gy[p], gx[p] = next_z - v, next_y - v, next_x - v
                    az[p], ay[p], ax[p] = v - prev_z, v - prev_y, v - prev_x
                h = [-(gz[p] + gy[p] + gx[p]) for p in range(2)]
                parts = [None] * FIELDS
                parts[ZZ] = az[0] * az[0] + az[1] * az[1]
                parts[YY] = ay[0] * ay[0] + ay[1] * ay[1]
                parts[XX] = ax[0] * ax[0] + ax[1] * ax[1]
                parts[CC] = h[0] * h[0] + h[1] * h[1]
                parts[Z0:Z0 + 2] = cmul(az, h)
                parts[ZY:ZY + 2] = cmul(az, ay)
                parts[ZX:ZX + 2] = cmul(az, ax)
                parts[Y0:Y0 + 2] = cmul(ay, h)
                parts[YX:YX + 2] = cmul(ay, ax)
                parts[C0X:C0X + 2] = cmul(h, ax)
                tot = parts if c == 0 else [a + b for a, b in zip(tot, parts)]
                t = [w * here[p] for p in range(2)]
                for g, wn, un in ((gz, w_z, uz), (gy, w_y, uy), (gx, w_x, ux)):
                    term = cmul(g, [t[p] - wn * un[p] for p in range(2)])
                    right = term if right is None else add(right, term)
            for n in range(FIELDS):
                macc[n, i] += tot[n]
            for p in range(2):
                bacc[p, i] += kap * right[p]

    def z_ready(s):
        @pl.when(below)
        def _():
            from_below(s).wait_recv()

        @pl.when(above)
        def _():
            from_above(s).wait_recv()

    def step(k, carry):
        s = lax.rem(f - k + nf, nf)
        before = lax.rem(f - k + 1 + nf, nf)
        for copy in arrivals(s):
            copy.wait_recv()
        forwards(s)
        z_ready(before)
        group(before)
        return carry

    lax.fori_loop(1, nf, step, 0)
    z_ready(fnext)
    group(fnext)

    for i in range(depth):
        for p in range(2):
            gath[0, f, p, i] = -bacc[p, i]

    def plane_sends(t):
        own = gath.at[t, f]
        return ((above, remote(own.at[:, depth - 1], mlo.at[t], pl_s.at[t, 0], pl_r.at[t, 0], f, zn)),
                (below, remote(own.at[:, 0], mhi.at[t], pl_s.at[t, 1], pl_r.at[t, 1], f, zp)),
                (diag_up, remote(own.at[:, depth - 1], mloc.at[t], pl_s.at[t, 2], pl_r.at[t, 2], f - 1, zn)),
                (diag_down, remote(own.at[:, 0], mhic.at[t], pl_s.at[t, 3], pl_r.at[t, 3], f + 1, zp)))

    def plane_arrivals(t):
        own = gath.at[t, f]
        return ((below, remote(own.at[:, depth - 1], mlo.at[t], pl_s.at[t, 0], pl_r.at[t, 0], f, zp)),
                (above, remote(own.at[:, 0], mhi.at[t], pl_s.at[t, 1], pl_r.at[t, 1], f, zn)),
                (diag_down, remote(own.at[:, depth - 1], mloc.at[t], pl_s.at[t, 2], pl_r.at[t, 2], f + 1, zp)),
                (diag_up, remote(own.at[:, 0], mhic.at[t], pl_s.at[t, 3], pl_r.at[t, 3], f - 1, zn)))

    def started(pairs):
        for cond, copy in pairs:
            pl.when(cond)(copy.start)

    def received(pairs):
        for cond, copy in pairs:
            pl.when(cond)(copy.wait_recv)

    def sent(pairs):
        for cond, copy in pairs:
            pl.when(cond)(copy.wait_send)

    order = []
    for k in range(1, nf // 2 + 1):
        order.append(k)
        if nf - k != k:
            order.append(nf - k)

    def tile_send(t, k):
        return remote(gath.at[t, f], gath.at[t, f], ag_s.at[t, k], ag_r.at[t, f], lax.rem(f + k, nf), z)

    def tile_from(t, s):
        return remote(gath.at[t, s], gath.at[t, s], ag_s.at[t, 0], ag_r.at[t, s], s, z)

    started(plane_sends(0))
    for k in order[:2]:
        tile_send(0, k).start()

    y_first = jnp.logical_and(lax.broadcasted_iota(jnp.int32, (rows, width), 0) == 0, f == 0)
    for i in range(depth):
        w = weight(i)
        zm = w * jnp.where(below, 1.0, 0.0).astype(jnp.float32) if i == 0 else w
        for n in range(FIELDS):
            val = macc[n, i] * (zm if n < YY else w)
            if n in (YY, Y0, Y0 + 1, YX, YX + 1, ZY, ZY + 1):
                val = jnp.where(y_first, 0.0, val)
            if n in (XX, ZX, ZX + 1, YX, YX + 1, C0X, C0X + 1):
                val = jnp.where(lane_first, 0.0, val)
            macc[n, i] = val
            if n in (ZY, ZY + 1):
                ysrc[5 + n - ZY, i:i + 1, :] = val[0:1]
            elif YY <= n < CC:
                ysrc[n - YY, i:i + 1, :] = val[0:1]

    mz_pair = ((below, remote(macc.at[0:YY, 0], mz, mz_sem.at[0], mz_sem.at[1], f, zp)),)
    mz_from = ((above, remote(macc.at[0:YY, 0], mz, mz_sem.at[0], mz_sem.at[1], f, zn)),)
    yp_pair = ((first, remote(ysrc, yp, yp_sem.at[0], yp_sem.at[1], fprev, z)),)
    yp_from = ((last, remote(ysrc, yp, yp_sem.at[0], yp_sem.at[1], fnext, z)),)
    started(mz_pair)
    started(yp_pair)
    for k in order[2:]:
        tile_send(0, k).start()

    def apply(t):
        rows_next = [gath[t, fnext, p, :, 0, :] for p in range(2)]
        rows_here = [gath[t, f, p, :, rows - 1, :] for p in range(2)]
        rows_z = [jnp.concatenate([mloc[t, p, 0:1, :], rows_next[p][:-1]], axis=0) for p in range(2)]
        rows_x = [lane_prev(rows_next[p]) for p in range(2)]
        vy_edge = add(scale(yp[0], rows_here), mul((yp[1], yp[2]), rows_next), mul((yp[3], yp[4]), rows_x),
                      cmul((yp[5], yp[6]), rows_z))
        m4 = [mhi[t, p] for p in range(2)]
        m4y = [shifted_down(m4[p], mhic[t, p, rows - 1:rows, :]) for p in range(2)]
        m4x = [lane_prev(m4[p]) for p in range(2)]
        m4z = [gath[t, f, p, depth - 1] for p in range(2)]
        vz_edge = add(scale(mz[ZZ], m4z), mul((mz[Z0], mz[Z0 + 1]), m4), mul((mz[ZY], mz[ZY + 1]), m4y),
                      mul((mz[ZX], mz[ZX + 1]), m4x))
        after = vz_edge
        for i in reversed(range(depth)):
            m = [gath[t, f, p, i] for p in range(2)]
            m_z = [gath[t, f, p, i - 1] if i > 0 else mlo[t, p] for p in range(2)]
            m_y = [shifted_down(m[p], gath[t, fprev, p, i, rows - 1:rows, :]) for p in range(2)]
            m_x = [lane_prev(m[p]) for p in range(2)]

            def pair(n):
                return macc[n, i], macc[n + 1, i]

            z0, zy, zx, y0, yx, cx = pair(Z0), pair(ZY), pair(ZX), pair(Y0), pair(YX), pair(C0X)
            v0 = add(scale(macc[CC, i], m), cmul(z0, m_z), cmul(y0, m_y), mul(cx, m_x))
            vx = add(scale(macc[XX, i], m_x), cmul(cx, m), cmul(zx, m_z), cmul(yx, m_y))
            vy = add(scale(macc[YY, i], m_y), mul(y0, m), mul(yx, m_x), cmul(zy, m_z))
            vz = add(scale(macc[ZZ, i], m_z), mul(z0, m), mul(zy, m_y), mul(zx, m_x))
            for p in range(2):
                gath[t + 1, f, p, i] = (v0[p] + lane_next(vx[p]) + shifted_up(vy[p], vy_edge[p][i:i + 1])
                                        + after[p] + DAMPING * m[p])
            after = vz

    def halo_ready(t):
        received(plane_arrivals(t))
        tile_from(t, fnext).wait_recv()
        tile_from(t, fprev).wait_recv()

    received(mz_from)
    received(yp_from)
    halo_ready(0)
    apply(0)
    started(plane_sends(1))
    for k in order:
        tile_send(1, k).start()

    def product(a, b):
        total = None
        for i in range(depth):
            for p in range(2):
                term = gath[a, f, p, i] * gath[b, f, p, i]
                total = term if total is None else total + term
        return jnp.sum(total, axis=0, keepdims=True)

    scs[0, 0:1, :] = product(0, 0)
    scs[0, 1:2, :] = product(0, 1)
    scs[0, 2:3, :] = product(1, 1)
    halo_ready(1)
    apply(1)
    scs[0, 3:4, :] = product(1, 2)

    def part_send(k):
        return remote(scs.at[0], scr.at[f], sc_s.at[k], sc_r.at[f], lax.rem(f + k, nf), z)

    for k in order:
        part_send(k).start()
    for k in order:
        tile_send(2, k).start()
    total = scs[0]
    for k in order:
        s = lax.rem(f - k + nf, nf)
        remote(scs.at[0], scr.at[s], sc_s.at[k], sc_r.at[s], s, z).wait_recv()
        total = total + scr[s]
    sgs[0] = total

    def sum_send(k):
        return remote(sgs.at[0], sgr.at[z], sg_s.at[k], sg_r.at[z], f, lax.rem(z + k, nz))

    for k in range(1, nz):
        sum_send(k).start()
    for k in range(1, nz):
        s = lax.rem(z - k + nz, nz)
        remote(sgs.at[0], sgr.at[s], sg_s.at[k], sg_r.at[s], f, s).wait_recv()
        total = total + sgr[s]
    sums = jnp.sum(total, axis=1, keepdims=True)
    bb, bq, qq, qs = (sums[n:n + 1, :] for n in range(4))
    alpha = bb / bq
    norm = bb - 2.0 * alpha * bq + alpha * alpha * qq
    beta = 1.0 + norm / bb
    second = norm / (beta * beta * bq - 2.0 * alpha * beta * qq + alpha * alpha * qs)
    c1 = jnp.broadcast_to(alpha + second * beta, (rows, width))
    c2 = jnp.broadcast_to(alpha * second, (rows, width))

    def finish(s):
        for p in range(2):
            for i in range(depth):
                b, q, r = gath[0, s, p, i], gath[1, s, p, i], gath[2, s, p, i]
                mod_out[p, i, s] = c1 * b - c2 * q
                res_out[p, i, s] = b - c1 * q + c2 * r

    finish(f)
    for k in order:
        s = lax.rem(f - k + nf, nf)
        if k not in (1, nf - 1):
            tile_from(0, s).wait_recv()
            tile_from(1, s).wait_recv()
        tile_from(2, s).wait_recv()
        finish(s)

    for k in range(1, nf):
        for copy in sends(lax.rem(f + k, nf)):
            copy.wait_send()
        for t in range(3):
            tile_send(t, k).wait_send()
        part_send(k).wait_send()
    for s in range(nf):
        pl.when(above)(forward_up(s).wait_send)
        pl.when(below)(forward_down(s).wait_send)
    pl.when(below)(w_copy.wait_send)
    sent(mz_pair)
    sent(yp_pair)
    for t in range(2):
        sent(plane_sends(t))
    for k in range(1, nz):
        sum_send(k).wait_send()


def body(nf, nz, displacement, freq_index, tissue):
    _, _, comps, depth, height, width = displacement.shape
    rows = height // nf
    u = displacement.reshape(2, comps, depth, nf, rows, width)
    tis = tissue.reshape(depth, nf, rows, width)
    f32 = jnp.float32
    dma = pltpu.SemaphoreType.DMA
    vmem = pl.BlockSpec(memory_space=pltpu.VMEM)
    out = jax.ShapeDtypeStruct((2, depth, nf, rows, width), f32)
    modulus, residual = pl.pallas_call(
        functools.partial(kernel, nf, nz),
        out_shape=(out, out),
        in_specs=[vmem, vmem, pl.BlockSpec(memory_space=pltpu.SMEM)],
        out_specs=(vmem, vmem),
        scratch_shapes=[
            pltpu.VMEM((nf, 2, comps, depth, rows, width), f32),
            pltpu.VMEM((nf, 2 * comps + 1, 2 * depth, width), f32),
            pltpu.VMEM((nf, 2 * comps + 1, 2 * depth, width), f32),
            pltpu.VMEM((nf, 2, comps, rows, width), f32),
            pltpu.VMEM((nf, 2, comps, rows, width), f32),
            pltpu.VMEM((rows, width), f32),
            pltpu.VMEM((rows, width), f32),
            pltpu.VMEM((FIELDS, depth, rows, width), f32),
            pltpu.VMEM((2, depth, rows, width), f32),
            pltpu.VMEM((YY, rows, width), f32),
            pltpu.VMEM((7, depth, width), f32),
            pltpu.VMEM((7, depth, width), f32),
            pltpu.VMEM((3, nf, 2, depth, rows, width), f32),
            pltpu.VMEM((2, 2, rows, width), f32),
            pltpu.VMEM((2, 2, rows, width), f32),
            pltpu.VMEM((2, 2, rows, width), f32),
            pltpu.VMEM((2, 2, rows, width), f32),
            pltpu.VMEM((1, 4, width), f32),
            pltpu.VMEM((nf, 4, width), f32),
            pltpu.VMEM((1, 4, width), f32),
            pltpu.VMEM((nz, 4, width), f32),
            dma((2,)), dma((nf,)), dma((nf,)), dma((nf,)), dma((nf,)),
            dma((nf,)), dma((nf,)), dma((nf,)), dma((nf,)),
            dma((2,)), dma((2,)), dma((2,)),
            dma((3, nf)), dma((3, nf)), dma((2, 4)), dma((2, 4)),
            dma((nf,)), dma((nf,)), dma((nz,)), dma((nz,)),
        ],
        compiler_params=pltpu.CompilerParams(collective_id=0, has_side_effects=True),
    )(u, tis, freq_index)
    shape = (2, depth, height, width)
    return modulus.reshape(shape), residual.reshape(shape)


def solution(mesh):
    placed = (P("freq", None, None, "gz", None, None), P("freq"), P("gz", None, None))
    return jax.shard_map(
        functools.partial(body, mesh.shape["freq"], mesh.shape["gz"]),
        mesh=mesh,
        in_specs=placed,
        out_specs=(P(None, "gz", None, None), P(None, "gz", None, None)),
        check_vma=False,
    )
```

time: 273 us -> 45.9 us (0.17)
  waiting for transfers between devices: 190 us -> 0 us
  Pallas kernels: 0 us -> 42 us
  blocking collectives: 33.6 us -> 0 us
  between operations: 18.7 us -> 1.29 us
  other arithmetic: 12.6 us -> 0 us
  starting transfers between devices: 12.6 us -> 0 us
    psum x3 -> x0, waiting for transfers between devices: 159 us -> none  [summed_all(): return lax.psum(local, 'freq')]
    pallas_call x0 -> x1, Pallas kernels: none -> 42 us  [body(): pl.pallas_call(functools.partial(kernel, nf, nz), out_shape=(out, out), i...]
    psum x3 -> x0, blocking collectives: 33.6 us -> none  [inner(): return lax.psum(jnp.sum(first * second), 'gz')]
    ppermute x6 -> x0, waiting for transfers between devices: 31.2 us -> none  [passed_along(): return lax.ppermute(array, axis, pairs)]
    ppermute x6 -> x0, starting transfers between devices: 12.5 us -> none  [passed_along(): return lax.ppermute(array, axis, pairs)]
    reduce_sum x11 -> x0, other arithmetic: 5.66 us -> none  [the longest x3 4.06 us: inner(): return lax.psum(jnp.sum(first * second), 'gz')]
    slice x16 -> x0, local copies, waits for them, and re-layouts: 3.7 us -> none  [the longest x12 2.64 us: ahead(): moved = lax.slice_in_dim(field, 1, field.shape[spatial], axis=spatial)]
    sub x7 -> x0, other arithmetic: 3.2 us -> none  [the longest x3 1.25 us: adjoint(): diff = values - ahead(values, spatial, tail)]
  transfers between devices with their start and end apart: 9 -> 0, of which waited for: 9 -> 0; matrix products, arithmetic and copies ran while one was open for 1% -> 0% of each run, Pallas kernels for 0% -> 0%
where the time goes in v1:
time: 45.9 us; the launch traced here: 45.7 us
  Pallas kernels  42 us (92%)
  local copies, waits for them, and re-layouts  2.42 us (5%)
  between operations  1.29 us (3%)
    pallas_call x1, Pallas kernels, body(): pl.pallas_call(functools.partial(kernel, nf, nz), out_shape=(out, out), i...  42 us
    unnamed x4, local copies, waits for them, and re-layouts  2.42 us

profile of v1, /device:TPU:0, one launch (start us, length us, event | category | flops | bytes accessed | tf_op | source)
XLA Modules:
  0.0 45.7 jit_solution(4327287097362810441)
XLA Ops:
  1.3 42.0 %shard_map.50 = (f32[2,4,8,8,128]{4,3,2,1,0:T(8,128)}, f32[2,4,8,8,128]{4,3,2,1,0:T(8,128)}) custom-call(f32[2,3,4,8,8,128]{5,4,3,2,1,0:T(8,128)} %bitcast.4, s32[4,8,8,128]{3,2,1,0:T(8,128)} %bitcast.7, s32[1]{0:T(128)S(6)} %copy.7.fi), custom_call_target="tpu_custom_call" | custom-call | tf_op jit(solution)/shard_map/pallas_call | solution.py:473
  43.3 0.0 copy-start
  43.3 1.7 %copy.8 = f32[2,4,64,128]{3,2,1,0:T(8,128)} copy(f32[2,4,64,128]{3,2,1,0:T(8,128)} %bitcast.6) | data formatting | bytes 524288
  45.0 0.0 copy-done
  45.0 0.7 %copy.9 = f32[2,4,64,128]{3,2,1,0:T(8,128)} copy(f32[2,4,64,128]{3,2,1,0:T(8,128)S(1)} %bitcast.5) | data formatting | bytes 524288
Async XLA Ops:
  43.3 1.7 %copy-start = (f32[2,4,8,8,128]{4,3,2,1,0:T(8,128)S(1)}, f32[2,4,8,8,128]{4,3,2,1,0:T(8,128)}, u32[]{:S(2)}) copy-start(f32[2,4,8,8,128]{4,3,2,1,0:T(8,128)} %get-tuple-element.5) | copy-start | bytes 786436

commit v2 on v1

--- a/solution.py
+++ b/solution.py
@@ -138,6 +138,12 @@
 
     pl.semaphore_wait(barrier, (nf - 1) + (nz - 1) + diag_up.astype(jnp.int32) + diag_down.astype(jnp.int32))
 
+    order = []
+    for k in range(1, nf // 2 + 1):
+        order.append(k)
+        if nf - k != k:
+            order.append(nf - k)
+
     def sends(d):
         return (remote(hsrc.at[d], hbuf.at[f], halo_s.at[d], halo_r.at[f], d, z),
                 remote(u.at[:, :, :, d], ubuf.at[f], main_s.at[d], main_r.at[f], d, z))
@@ -146,9 +152,9 @@
         return (remote(hsrc.at[s], hbuf.at[s], halo_s.at[s], halo_r.at[s], s, z),
                 remote(u.at[:, :, :, s], ubuf.at[s], main_s.at[s], main_r.at[s], s, z))
 
-    for k in range(1, nf):
-        for copy in sends(lax.rem(f + k, nf)):
-            copy.start()
+    for part in (1, 0):
+        for k in order:
+            sends(lax.rem(f + k, nf))[part].start()
 
     w_copy = remote(wsrc, wz, w_sem.at[0], w_sem.at[1], f, zp)
     w_from = remote(wsrc, wz, w_sem.at[0], w_sem.at[1], f, zn)
@@ -249,19 +255,22 @@
         def _():
             from_above(s).wait_recv()
 
+    for k in order:
+        s = lax.rem(f - k + nf, nf)
+        arrivals(s)[1].wait_recv()
+        forwards(s)
+
+    z_ready(f)
+    group(f)
+
     def step(k, carry):
         s = lax.rem(f - k + nf, nf)
-        before = lax.rem(f - k + 1 + nf, nf)
-        for copy in arrivals(s):
-            copy.wait_recv()
-        forwards(s)
-        z_ready(before)
-        group(before)
+        arrivals(s)[0].wait_recv()
+        z_ready(s)
+        group(s)
         return carry
 
     lax.fori_loop(1, nf, step, 0)
-    z_ready(fnext)
-    group(fnext)
 
     for i in range(depth):
         for p in range(2):
@@ -292,12 +301,6 @@
     def sent(pairs):
         for cond, copy in pairs:
             pl.when(cond)(copy.wait_send)
-
-    order = []
-    for k in range(1, nf // 2 + 1):
-        order.append(k)
-        if nf - k != k:
-            order.append(nf - k)
 
     def tile_send(t, k):
         return remote(gath.at[t, f], gath.at[t, f], ag_s.at[t, k], ag_r.at[t, f], lax.rem(f + k, nf), z)
@@ -376,55 +379,69 @@
     received(yp_from)
     halo_ready(0)
     apply(0)
+
+    def exchange_over_freq(n, values):
+        for row, value in enumerate(values):
+            scs[n, row:row + 1, :] = jnp.sum(value, axis=0, keepdims=True)
+        for k in order:
+            part_send(n, k).start()
+
+    def exchange_over_gz(n):
+        total = scs[n]
+        for k in order:
+            s = lax.rem(f - k + nf, nf)
+            remote(scs.at[n], scr.at[n, s], sc_s.at[n, k], sc_r.at[n, s], s, z).wait_recv()
+            total = total + scr[n, s]
+        sgs[n] = total
+        for k in range(1, nz):
+            sum_send(n, k).start()
+
+    def exchanged(n):
+        total = sgs[n]
+        for k in range(1, nz):
+            s = lax.rem(z - k + nz, nz)
+            remote(sgs.at[n], sgr.at[n, s], sg_s.at[n, k], sg_r.at[n, s], f, s).wait_recv()
+            total = total + sgr[n, s]
+        sums = jnp.sum(total, axis=1, keepdims=True)
+        return [sums[row:row + 1, :] for row in range(4)]
+
+    def part_send(n, k):
+        return remote(scs.at[n], scr.at[n, f], sc_s.at[n, k], sc_r.at[n, f], lax.rem(f + k, nf), z)
+
+    def sum_send(n, k):
+        return remote(sgs.at[n], sgr.at[n, z], sg_s.at[n, k], sg_r.at[n, z], f, lax.rem(z + k, nz))
+
+    def inner(pairs):
+        return sum(a * b for a, b in pairs)
+
+    def tiles(t):
+        return [gath[t, f, p, i] for p in range(2) for i in range(depth)]
+
     started(plane_sends(1))
-    for k in order:
+    for k in order[:2]:
         tile_send(1, k).start()
-
-    def product(a, b):
-        total = None
-        for i in range(depth):
-            for p in range(2):
-                term = gath[a, f, p, i] * gath[b, f, p, i]
-                total = term if total is None else total + term
-        return jnp.sum(total, axis=0, keepdims=True)
-
-    scs[0, 0:1, :] = product(0, 0)
-    scs[0, 1:2, :] = product(0, 1)
-    scs[0, 2:3, :] = product(1, 1)
+    scs[...] = jnp.zeros_like(scs)
+    right, image = tiles(0), tiles(1)
+    exchange_over_freq(0, (inner(zip(right, right)), inner(zip(right, image))))
+    for k in order[2:]:
+        tile_send(1, k).start()
+    exchange_over_gz(0)
     halo_ready(1)
     apply(1)
-    scs[0, 3:4, :] = product(1, 2)
-
-    def part_send(k):
-        return remote(scs.at[0], scr.at[f], sc_s.at[k], sc_r.at[f], lax.rem(f + k, nf), z)
-
-    for k in order:
-        part_send(k).start()
+    bb, bq = exchanged(0)[:2]
+    alpha = bb / bq
+    step_size = jnp.broadcast_to(alpha, (rows, width))
+    right, image = tiles(0), tiles(1)
+    left = [b - step_size * q for b, q in zip(right, image)]
+    exchange_over_freq(1, (inner(zip(left, left)), inner(zip(left, image)),
+                           inner((r, q - step_size * s) for r, q, s in zip(left, image, tiles(2)))))
     for k in order:
         tile_send(2, k).start()
-    total = scs[0]
-    for k in order:
-        s = lax.rem(f - k + nf, nf)
-        remote(scs.at[0], scr.at[s], sc_s.at[k], sc_r.at[s], s, z).wait_recv()
-        total = total + scr[s]
-    sgs[0] = total
-
-    def sum_send(k):
-        return remote(sgs.at[0], sgr.at[z], sg_s.at[k], sg_r.at[z], f, lax.rem(z + k, nz))
-
-    for k in range(1, nz):
-        sum_send(k).start()
-    for k in range(1, nz):
-        s = lax.rem(z - k + nz, nz)
-        remote(sgs.at[0], sgr.at[s], sg_s.at[k], sg_r.at[s], f, s).wait_recv()
-        total = total + sgr[s]
-    sums = jnp.sum(total, axis=1, keepdims=True)
-    bb, bq, qq, qs = (sums[n:n + 1, :] for n in range(4))
-    alpha = bb / bq
-    norm = bb - 2.0 * alpha * bq + alpha * alpha * qq
-    beta = 1.0 + norm / bb
-    second = norm / (beta * beta * bq - 2.0 * alpha * beta * qq + alpha * alpha * qs)
-    c1 = jnp.broadcast_to(alpha + second * beta, (rows, width))
+    exchange_over_gz(1)
+    rr, rq, rnr = exchanged(1)[:3]
+    ratio = rr / bb
+    second = rr / (rnr + 2.0 * ratio * rq + ratio * ratio * bq)
+    c1 = jnp.broadcast_to(alpha + second * (1.0 + ratio), (rows, width))
     c2 = jnp.broadcast_to(alpha * second, (rows, width))
 
     def finish(s):
@@ -448,7 +465,8 @@
             copy.wait_send()
         for t in range(3):
             tile_send(t, k).wait_send()
-        part_send(k).wait_send()
+        for n in range(2):
+            part_send(n, k).wait_send()
     for s in range(nf):
         pl.when(above)(forward_up(s).wait_send)
         pl.when(below)(forward_down(s).wait_send)
@@ -458,7 +476,8 @@
     for t in range(2):
         sent(plane_sends(t))
     for k in range(1, nz):
-        sum_send(k).wait_send()
+        for n in range(2):
+            sum_send(n, k).wait_send()
 
 
 def body(nf, nz, displacement, freq_index, tissue):
@@ -493,15 +512,15 @@
             pltpu.VMEM((2, 2, rows, width), f32),
             pltpu.VMEM((2, 2, rows, width), f32),
             pltpu.VMEM((2, 2, rows, width), f32),
-            pltpu.VMEM((1, 4, width), f32),
-            pltpu.VMEM((nf, 4, width), f32),
-            pltpu.VMEM((1, 4, width), f32),
-            pltpu.VMEM((nz, 4, width), f32),
+            pltpu.VMEM((2, 4, width), f32),
+            pltpu.VMEM((2, nf, 4, width), f32),
+            pltpu.VMEM((2, 4, width), f32),
+            pltpu.VMEM((2, nz, 4, width), f32),
             dma((2,)), dma((nf,)), dma((nf,)), dma((nf,)), dma((nf,)),
             dma((nf,)), dma((nf,)), dma((nf,)), dma((nf,)),
             dma((2,)), dma((2,)), dma((2,)),
             dma((3, nf)), dma((3, nf)), dma((2, 4)), dma((2, 4)),
-            dma((nf,)), dma((nf,)), dma((nz,)), dma((nz,)),
+            dma((2, nf)), dma((2, nf)), dma((2, nz)), dma((2, nz)),
         ],
         compiler_params=pltpu.CompilerParams(collective_id=0, has_side_effects=True),
     )(u, tis, freq_index)

time: 45.9 us -> 45.6 us (level)
  no operation moved by 1% of the time
where the time goes in v2:
time: 45.6 us; the launch traced here: 45.5 us
  Pallas kernels  41.7 us (91%)
  local copies, waits for them, and re-layouts  2.42 us (5%)
  between operations  1.29 us (3%)
    pallas_call x1, Pallas kernels, body(): pl.pallas_call(functools.partial(kernel, nf, nz), out_shape=(out, out), i...  41.7 us
    unnamed x4, local copies, waits for them, and re-layouts  2.42 us

profile of v2, /device:TPU:0, one launch (start us, length us, event | category | flops | bytes accessed | tf_op | source)
XLA Modules:
  0.0 45.5 jit_solution(1198803917396433690)
XLA Ops:
  1.3 41.7 %shard_map.50 = (f32[2,4,8,8,128]{4,3,2,1,0:T(8,128)}, f32[2,4,8,8,128]{4,3,2,1,0:T(8,128)}) custom-call(f32[2,3,4,8,8,128]{5,4,3,2,1,0:T(8,128)} %bitcast.4, s32[4,8,8,128]{3,2,1,0:T(8,128)} %bitcast.7, s32[1]{0:T(128)S(6)} %copy.7.fi), custom_call_target="tpu_custom_call" | custom-call | tf_op jit(solution)/shard_map/pallas_call | solution.py:492
  43.0 0.0 copy-start
  43.0 1.7 %copy.8 = f32[2,4,64,128]{3,2,1,0:T(8,128)} copy(f32[2,4,64,128]{3,2,1,0:T(8,128)} %bitcast.6) | data formatting | bytes 524288
  44.8 0.0 copy-done
  44.8 0.7 %copy.9 = f32[2,4,64,128]{3,2,1,0:T(8,128)} copy(f32[2,4,64,128]{3,2,1,0:T(8,128)S(1)} %bitcast.5) | data formatting | bytes 524288
Async XLA Ops:
  43.0 1.7 %copy-start = (f32[2,4,8,8,128]{4,3,2,1,0:T(8,128)S(1)}, f32[2,4,8,8,128]{4,3,2,1,0:T(8,128)}, u32[]{:S(2)}) copy-start(f32[2,4,8,8,128]{4,3,2,1,0:T(8,128)} %get-tuple-element.5) | copy-start | bytes 786436

commit v3 on v2

--- a/solution.py
+++ b/solution.py
@@ -418,30 +418,22 @@
         return [gath[t, f, p, i] for p in range(2) for i in range(depth)]
 
     started(plane_sends(1))
-    for k in order[:2]:
+    for k in order:
         tile_send(1, k).start()
-    scs[...] = jnp.zeros_like(scs)
     right, image = tiles(0), tiles(1)
-    exchange_over_freq(0, (inner(zip(right, right)), inner(zip(right, image))))
-    for k in order[2:]:
-        tile_send(1, k).start()
-    exchange_over_gz(0)
+    moments = [inner(zip(right, right)), inner(zip(right, image)), inner(zip(image, image))]
     halo_ready(1)
     apply(1)
-    bb, bq = exchanged(0)[:2]
-    alpha = bb / bq
-    step_size = jnp.broadcast_to(alpha, (rows, width))
-    right, image = tiles(0), tiles(1)
-    left = [b - step_size * q for b, q in zip(right, image)]
-    exchange_over_freq(1, (inner(zip(left, left)), inner(zip(left, image)),
-                           inner((r, q - step_size * s) for r, q, s in zip(left, image, tiles(2)))))
+    exchange_over_freq(0, moments + [inner(zip(image, tiles(2)))])
     for k in order:
         tile_send(2, k).start()
-    exchange_over_gz(1)
-    rr, rq, rnr = exchanged(1)[:3]
-    ratio = rr / bb
-    second = rr / (rnr + 2.0 * ratio * rq + ratio * ratio * bq)
-    c1 = jnp.broadcast_to(alpha + second * (1.0 + ratio), (rows, width))
+    exchange_over_gz(0)
+    bb, bq, qq, qs = exchanged(0)
+    alpha = bb / bq
+    norm = bb - 2.0 * alpha * bq + alpha * alpha * qq
+    beta = 1.0 + norm / bb
+    second = norm / (beta * beta * bq - 2.0 * alpha * beta * qq + alpha * alpha * qs)
+    c1 = jnp.broadcast_to(alpha + second * beta, (rows, width))
     c2 = jnp.broadcast_to(alpha * second, (rows, width))
 
     def finish(s):
@@ -465,8 +457,7 @@
             copy.wait_send()
         for t in range(3):
             tile_send(t, k).wait_send()
-        for n in range(2):
-            part_send(n, k).wait_send()
+        part_send(0, k).wait_send()
     for s in range(nf):
         pl.when(above)(forward_up(s).wait_send)
         pl.when(below)(forward_down(s).wait_send)
@@ -476,8 +467,7 @@
     for t in range(2):
         sent(plane_sends(t))
     for k in range(1, nz):
-        for n in range(2):
-            sum_send(n, k).wait_send()
+        sum_send(0, k).wait_send()
 
 
 def body(nf, nz, displacement, freq_index, tissue):

time: 45.6 us -> 41.6 us (0.912)
  Pallas kernels: 41.7 us -> 37.7 us
    pallas_call x1, Pallas kernels: 41.7 us -> 37.7 us  [body(): pl.pallas_call(functools.partial(kernel, nf, nz), out_shape=(out, out), i...]
where the time goes in v3:
time: 41.6 us; the launch traced here: 41.4 us
  Pallas kernels  37.7 us (91%)
  local copies, waits for them, and re-layouts  2.42 us (6%)
  between operations  1.29 us (3%)
    pallas_call x1, Pallas kernels, body(): pl.pallas_call(functools.partial(kernel, nf, nz), out_shape=(out, out), i...  37.7 us
    unnamed x4, local copies, waits for them, and re-layouts  2.42 us

profile of v3, /device:TPU:0, one launch (start us, length us, event | category | flops | bytes accessed | tf_op | source)
XLA Modules:
  0.0 41.4 jit_solution(555310245522494644)
XLA Ops:
  1.3 37.7 %shard_map.50 = (f32[2,4,8,8,128]{4,3,2,1,0:T(8,128)}, f32[2,4,8,8,128]{4,3,2,1,0:T(8,128)}) custom-call(f32[2,3,4,8,8,128]{5,4,3,2,1,0:T(8,128)} %bitcast.4, s32[4,8,8,128]{3,2,1,0:T(8,128)} %bitcast.7, s32[1]{0:T(128)S(6)} %copy.7.fi), custom_call_target="tpu_custom_call" | custom-call | tf_op jit(solution)/shard_map/pallas_call | solution.py:482
  39.0 0.0 copy-start
  39.0 1.7 %copy.8 = f32[2,4,64,128]{3,2,1,0:T(8,128)} copy(f32[2,4,64,128]{3,2,1,0:T(8,128)} %bitcast.6) | data formatting | bytes 524288
  40.7 0.0 copy-done
  40.7 0.7 %copy.9 = f32[2,4,64,128]{3,2,1,0:T(8,128)} copy(f32[2,4,64,128]{3,2,1,0:T(8,128)S(1)} %bitcast.5) | data formatting | bytes 524288
Async XLA Ops:
  39.0 1.7 %copy-start = (f32[2,4,8,8,128]{4,3,2,1,0:T(8,128)S(1)}, f32[2,4,8,8,128]{4,3,2,1,0:T(8,128)}, u32[]{:S(2)}) copy-start(f32[2,4,8,8,128]{4,3,2,1,0:T(8,128)} %get-tuple-element.5) | copy-start | bytes 786436
